TPU v7x, 32 devices: a whole 2x2x4 slice. The times are simulated.
32 devices in a mesh: atom: 16 (over z, y, core), band: 2 (over x).
Axes of the slice: x: 2, y: 2, z: 4, core: 2. Of those that a mesh axis runs over, the one named last changes fastest.
Arguments:
- wave_rows: bfloat16 [256, 65536], P('atom', 'band'), may hold values from -6 to 6
- projectors: bfloat16 [2048, 65536], P('atom', 'band'), may hold values from -0.0234375 to 0.0234375
- dij_table: float32 [16, 8, 8], replicated, may hold values from -6 to 6
- dij_index: int32 [256], P('atom'), may hold values from 0 to 15
- proj_count: int32 [256], P('atom'), may hold values from 1 to 8
Outputs:
- nonlocal_rows: bfloat16 [256, 65536], P('atom', 'band')
All inputs are finite; a program needn't handle non-finite values.
Results may differ from a plain program's by a relative error of at most 0.0049.
Values may be sent and summed in bfloat16 or wider, within the bound.
No kernel may reach another device: no remote copies, remote signals or barrier semaphores. Data moves between devices by JAX's collectives and lax.ppermute only.
A program may use at most 128 MiB of HBM per device.

v0:
```python
import jax
import jax.numpy as jnp
from jax import lax
from jax.sharding import PartitionSpec as P


def shards(wave_rows, projectors, dij_table, dij_index, proj_count):
    atom_local = dij_index.shape[0]
    kind_total = dij_table.shape[0]
    per_atom = dij_table.shape[1]
    width = atom_local * per_atom
    partial_value = lax.dot_general(
        lax.all_gather(wave_rows, "atom", axis=0, tiled=True),
        projectors,
        (((1,), (1,)), ((), ())),
        preferred_element_type=jnp.float32,
    )
    kind_onehot = (dij_index[:, None] == jnp.arange(kind_total, dtype=jnp.int32)[None, :]).astype(
        jnp.float32
    )
    blocks = jnp.dot(
        kind_onehot,
        dij_table.reshape(kind_total, per_atom * per_atom),
        precision=lax.Precision.HIGHEST,
    ).reshape(atom_local, per_atom, per_atom)
    active = (jnp.arange(per_atom, dtype=jnp.int32)[None, :] < proj_count[:, None]).astype(
        jnp.float32
    )
    blocks = blocks * active[:, :, None] * active[:, None, :]
    share = lax.psum_scatter(partial_value, "band", scatter_dimension=0, tiled=True)
    count = share.shape[0]
    mixed = jnp.einsum(
        "baj,aij->bai",
        share.reshape(count, atom_local, per_atom),
        blocks,
        precision=lax.Precision.HIGHEST,
    )
    weighted = lax.all_gather(
        mixed.reshape(count, width).astype(jnp.bfloat16), "band", axis=0, tiled=True
    )
    result = lax.psum_scatter(
        jnp.dot(weighted, projectors, preferred_element_type=jnp.float32),
        "atom",
        scatter_dimension=0,
        tiled=True,
    )
    return result.astype(jnp.bfloat16)


def solution(mesh):
    in_specs = (P("atom", "band"), P("atom", "band"), P(), P("atom"), P("atom"))
    out_specs = P("atom", "band")
    return jax.shard_map(shards, mesh=mesh, in_specs=in_specs, out_specs=out_specs, check_vma=False)
```

profile of v0, /device:TPU:0, one launch (start us, length us, event | category | flops | bytes accessed | tf_op | source)
XLA Modules:
  0.0 523.0 jit_solution(4705816318963149127)
XLA Ops:
  6.5 0.0 copy-start
  6.5 0.0 all-gather.2.cloned.1.call-start
  6.5 0.7 all-gather.2.cloned.1.call-update
  7.3 0.0 copy-start.1
  7.3 0.0 copy-start.2
  7.3 0.0 reduce-scatter.3.cloned.1.call-start
  7.3 131.4 %all-gather.2.cloned.1.call-done = bf16[256,32768]{1,0:T(8,128)(2,1)} async-done(((bf16[16,32768]{1,0:T(8,128)(2,1)}), bf16[256,32768]{1,0:T(8,128)(2,1)}) %all-gather.2.cloned.1.call-update) | async-done | bytes 16777232 | tf_op jit(solution)/shard_map/all_gather | solution.py:13
  138.7 13.3 %fusion.12 = f32[256,128]{1,0:T(8,128)} fusion(bf16[256,32768]{1,0:T(8,128)(2,1)} %all-gather.2.cloned.1.call-done, bf16[128,32768]{1,0:T(8,128)(2,1)} %param.6), kind=kOutput, calls=%fused_computation.14 | convolution fusion | flops 2147483648 | bytes 25296896 | tf_op jit(solution)/shard_map/dot_general | solution.py:12
  152.0 0.0 reduce-scatter.3.cloned.1.call-update
  152.0 0.0 reduce-scatter.5.cloned.1.call-start
  152.0 0.0 copy-done
  152.1 0.0 copy-done.1
  152.1 0.2 fusion.4
  152.3 0.1 copy.8
  152.4 0.0 copy-done.2
  152.4 0.1 fusion.10
  152.5 8.2 %reduce-scatter.3.cloned.1.call-done = f32[128,128]{1,0:T(8,128)} async-done(((f32[256,128]{1,0:T(8,128)}), f32[128,128]{1,0:T(8,128)}) %reduce-scatter.3.cloned.1.call-update) | async-done | bytes 65552 | tf_op jit(solution)/shard_map/reduce_scatter | solution.py:30
  160.7 0.9 copy.7
  161.6 0.3 fusion
  162.0 4.6 all_gather.7
  166.6 16.5 %fusion.13 = f32[256,32768]{1,0:T(8,128)} fusion(bf16[256,128]{0,1:T(8,128)(2,1)S(1)} %all_gather.7, bf16[128,32768]{1,0:T(8,128)(2,1)} %param.6), kind=kOutput, calls=%fused_computation.15 | convolution fusion | flops 2147483648 | bytes 42008576 | tf_op jit(solution)/shard_map/dot_general | solution.py:42
  183.1 0.0 reduce-scatter.5.cloned.1.call-update
  183.1 330.7 %reduce-scatter.5.cloned.1.call-done = f32[16,32768]{1,0:T(8,128)} async-done(((f32[256,32768]{1,0:T(8,128)}), f32[16,32768]{1,0:T(8,128)}) %reduce-scatter.5.cloned.1.call-update) | async-done | bytes 2097168 | tf_op jit(solution)/shard_map/reduce_scatter | solution.py:41
  513.8 2.7 convert_element_type.28
Async XLA Ops:
  6.5 145.5 %copy-start = (f32[16,8,8]{0,2,1:T(8,128)S(1)}, f32[16,8,8]{0,2,1:T(8,128)}, u32[]{:S(2)}) copy-start(f32[16,8,8]{0,2,1:T(8,128)} %param.7) | copy-start | bytes 12292
  6.5 132.1 %all-gather.2.cloned.1.call-start = ((), (), s32[]{:S(2)}) async-start(), calls=%async_computation.2 | async-start | bytes 17825792 | tf_op jit(solution)/shard_map/all_gather | solution.py:13
  7.3 144.8 %copy-start.1 = (s32[16]{0:T(128)S(1)}, s32[16]{0:T(128)}, u32[]{:S(2)}) copy-start(s32[16]{0:T(128)} %param.8) | copy-start | bytes 196
  7.3 145.1 %copy-start.2 = (s32[16]{0:T(128)S(1)}, s32[16]{0:T(128)}, u32[]{:S(2)}) copy-start(s32[16]{0:T(128)} %param.9) | copy-start | bytes 196
  7.3 153.4 %reduce-scatter.3.cloned.1.call-start = ((), (), s32[]{:S(2)}) async-start(), calls=%async_computation.3 | async-start | bytes 196608 | tf_op jit(solution)/shard_map/reduce_scatter | solution.py:30
  152.0 361.8 %reduce-scatter.5.cloned.1.call-start = ((), (), s32[]{:S(2)}) async-start(), calls=%async_computation.4 | async-start | bytes 35651584 | tf_op jit(solution)/shard_map/reduce_scatter | solution.py:41
Sparse Core Ops, SparseCore 0:
  9.5 129.1 all-gather.1
  152.1 8.5 reduce-scatter.2
  183.2 330.5 reduce-scatter.4
where the time goes:
time: 523 us
  waiting for transfers between devices  471 us (90%)
  matrix products  30.3 us (6%)
  between operations  13.2 us (3%)
    reduce_scatter x1, waiting for transfers between devices, shards(): lax.psum_scatter(jnp.dot(weighted, projectors, preferred_element_type=jnp...  331 us
    all_gather x1, waiting for transfers between devices, shards(): lax.all_gather(wave_rows, 'atom', axis=0, tiled=True)  131 us
    dot_general x1, matrix products, shards(): jnp.dot(weighted, projectors, preferred_element_type=jnp.float32)  16.5 us
    dot_general x1, matrix products, shards(): lax.dot_general(lax.all_gather(wave_rows, 'atom', axis=0, tiled=True), pr...  13.3 us
  transfers between devices with their start and end apart: 3, of which 3 were waited for; matrix products, arithmetic and copies ran while one was open for 0% of the time, Pallas kernels for 0%

commit v1 on v0

v1 whole, which is shorter than its diff:
```python
import jax
import jax.numpy as jnp
from jax import lax
from jax.sharding import Mesh
from jax.sharding import PartitionSpec as P


def block_diagonal(dij_table, dij_index, proj_count):
    atom_local = dij_index.shape[0]
    kind_total, per_atom = dij_table.shape[0], dij_table.shape[1]
    kind_onehot = (dij_index[:, None] == jnp.arange(kind_total, dtype=jnp.int32)[None, :]).astype(
        jnp.float32
    )
    blocks = jnp.dot(
        kind_onehot,
        dij_table.reshape(kind_total, per_atom * per_atom),
        precision=lax.Precision.HIGHEST,
    ).reshape(atom_local, per_atom, per_atom)
    active = (jnp.arange(per_atom, dtype=jnp.int32)[None, :] < proj_count[:, None]).astype(
        jnp.float32
    )
    blocks = blocks * active[:, :, None] * active[:, None, :]
    same = jnp.eye(atom_local, dtype=jnp.float32)
    spread = jnp.swapaxes(blocks, 1, 2)[:, :, None, :] * same[:, None, :, None]
    return spread.reshape(atom_local * per_atom, atom_local * per_atom)


def solution(mesh):
    atoms, bands = mesh.shape["atom"], mesh.shape["band"]
    lo = 4 if atoms % 4 == 0 else 1
    hi = atoms // lo
    grid = Mesh(mesh.devices.reshape(hi, lo, bands), ("hi", "lo", "band"))

    def swap(x, axis, size, step):
        return lax.ppermute(x, axis, [(k, k ^ step) for k in range(size)])

    def shift(x, step):
        return lax.ppermute(x, "hi", [(k, (k + step) % hi) for k in range(hi)])

    def shards(wave_rows, projectors, dij_table, dij_index, proj_count):
        rows, cols = wave_rows.shape
        span = cols // lo
        half = span // 2
        me = lax.axis_index("lo")

        def piece(x, step):
            return lax.dynamic_slice_in_dim(x, (me ^ step) * span, span, axis=1)

        parts = [piece(wave_rows, step) for step in range(lo)]
        for step in range(1, lo):
            parts[step] = swap(parts[step], "lo", lo, step)
        pieces = [piece(projectors, step) for step in range(lo)]
        wave_block = jnp.zeros((lo * rows, span), wave_rows.dtype)
        for step in range(lo):
            wave_block = lax.dynamic_update_slice_in_dim(
                wave_block, parts[step], (me ^ step) * rows, axis=0
            )
        proj = [pieces[0]]
        for step in range(1, lo):
            proj.append(swap(pieces[step], "lo", lo, step))
        stack = jnp.concatenate(proj, axis=0)
        group = lo * rows
        sides = []
        for side, way in ((0, 1), (1, -1)):
            block = wave_block[:, side * half : (side + 1) * half]
            whole = jnp.zeros((hi * group, half), wave_rows.dtype)
            whole = lax.dynamic_update_slice(whole, block, (0, 0))
            for t in range(1, hi):
                block = shift(block, way)
                whole = lax.dynamic_update_slice(whole, block, (way * t % hi * group, 0))
            sides.append(whole)

        def overlap(step):
            return sum(
                lax.dot_general(
                    sides[side],
                    proj[step][:, side * half : (side + 1) * half],
                    (((1,), (1,)), ((), ())),
                    preferred_element_type=jnp.float32,
                )
                for side in range(2)
            )

        total = overlap(0)
        for step in range(1, lo):
            total = total + swap(overlap(step), "lo", lo, step)
        if bands & (bands - 1) == 0:
            step = 1
            while step < bands:
                total = total + swap(total, "band", bands, step)
                step *= 2
        else:
            total = lax.psum(total, "band")
        mixed = jnp.dot(
            total,
            block_diagonal(dij_table, dij_index, proj_count),
            precision=lax.Precision.HIGHEST,
        ).astype(jnp.bfloat16)
        weighted = jnp.concatenate(
            [mixed] + [swap(mixed, "lo", lo, step) for step in range(1, lo)], axis=1
        )

        quarter = half // 2

        def contribution(r, side, sub):
            at = side * half + sub * quarter
            return jnp.dot(
                weighted[r * group : (r + 1) * group],
                stack[:, at : at + quarter],
                preferred_element_type=jnp.float32,
            )

        streams = [(sub, side, 1 - 2 * side) for sub in range(2) for side in range(2)]
        acc = [contribution(way % hi, side, sub) for sub, side, way in streams]
        for t in range(1, hi):
            moved = []
            for a, (sub, side, way) in zip(acc, streams):
                moved.append(shift(a.astype(jnp.bfloat16), way))
            acc = [
                contribution(way * (1 + t) % hi, side, sub) + m.astype(jnp.float32)
                for m, (sub, side, way) in zip(moved, streams)
            ]
        acc = [a.astype(jnp.bfloat16) for a in acc]
        result = jnp.zeros((rows, cols), jnp.bfloat16)
        for sub in range(2):
            own = jnp.concatenate(acc[2 * sub : 2 * sub + 2], axis=1)
            for step in range(lo):
                part = lax.dynamic_slice_in_dim(own, (me ^ step) * rows, rows, axis=0)
                if step:
                    part = swap(part, "lo", lo, step)
                for side in range(2):
                    result = lax.dynamic_update_slice_in_dim(
                        result,
                        part[:, side * quarter : (side + 1) * quarter],
                        (me ^ step) * span + side * half + sub * quarter,
                        axis=1,
                    )
        return result

    spec = P(("hi", "lo"), "band")
    index_spec = P(("hi", "lo"))

    return jax.shard_map(
        shards,
        mesh=grid,
        in_specs=(spec, spec, P(), index_spec, index_spec),
        out_specs=spec,
        check_vma=False,
    )
```

time: 523 us -> 222 us (0.42)
  waiting for transfers between devices: 471 us -> 115 us
  starting transfers between devices: 0.08 us -> 61.6 us
  local copies, waits for them, and re-layouts: 1.02 us -> 15.6 us
  between operations: 13.2 us -> 0.63 us
  matrix products: 30.3 us -> 24.7 us
    reduce_scatter x2 -> x0, waiting for transfers between devices: 339 us -> none  [the longest x1 331 us: shards(): lax.psum_scatter(jnp.dot(weighted, projectors, preferred_element_type=jnp...]
    all_gather x1 -> x0, waiting for transfers between devices: 131 us -> none  [shards(): lax.all_gather(wave_rows, 'atom', axis=0, tiled=True)]
    ppermute x0 -> x37, waiting for transfers between devices: none -> 115 us  [the longest x18 92.1 us: shift(): return lax.ppermute(x, 'hi', [(k, (k + step) % hi) for k in range(hi)])]
    ppermute x0 -> x37, starting transfers between devices: none -> 61.6 us  [the longest x18 46 us: shift(): return lax.ppermute(x, 'hi', [(k, (k + step) % hi) for k in range(hi)])]
    dynamic_slice x0 -> x2, local copies, waits for them, and re-layouts: none -> 8.39 us  [piece(): return lax.dynamic_slice_in_dim(x, (me ^ step) * span, span, axis=1)]
    dot_general x4 -> x26, matrix products: 30.3 us -> 24.7 us  [the longest x8 15.5 us: overlap(): lax.dot_general(sides[side], proj[step][:, side * half:(side + 1) * half]...]
  transfers between devices with their start and end apart: 3 -> 37, of which waited for: 3 -> 24; matrix products, arithmetic and copies ran while one was open for 0% -> 16% of each run, Pallas kernels for 0% -> 0%
where the time goes in v1:
time: 222 us; the launch traced here: 221 us
  waiting for transfers between devices  115 us (52%)
  starting transfers between devices  61.6 us (28%)
  matrix products  24.7 us (11%)
  local copies, waits for them, and re-layouts  15.6 us (7%)
  other arithmetic  4.08 us (2%)
    ppermute x18, waiting for transfers between devices, shift(): return lax.ppermute(x, 'hi', [(k, (k + step) % hi) for k in range(hi)])  92.1 us
    ppermute x18, starting transfers between devices, shift(): return lax.ppermute(x, 'hi', [(k, (k + step) % hi) for k in range(hi)])  46 us
    ppermute x19, waiting for transfers between devices, swap(): return lax.ppermute(x, axis, [(k, k ^ step) for k in range(size)])  22.8 us
    ppermute x19, starting transfers between devices, swap(): return lax.ppermute(x, axis, [(k, k ^ step) for k in range(size)])  15.6 us
    dot_general x8, matrix products, overlap(): lax.dot_general(sides[side], proj[step][:, side * half:(side + 1) * half]...  15.5 us
    dot_general x16, matrix products, contribution(): jnp.dot(weighted[r * group:(r + 1) * group], stack[:, at:at + quarter], p...  8.64 us
    dynamic_slice x2, local copies, waits for them, and re-layouts, piece(): return lax.dynamic_slice_in_dim(x, (me ^ step) * span, span, axis=1)  8.39 us
  transfers between devices with their start and end apart: 37, of which 24 were waited for; matrix products, arithmetic and copies ran while one was open for 16% of the time, Pallas kernels for 0%

profile of v1, /device:TPU:0, one launch (start us, length us, event | category | flops | bytes accessed | tf_op | source)
XLA Modules:
  0.0 221.5 jit_solution(11707720419196132107)
XLA Ops:
  0.1 2.1 constant_dynamic-slice_fusion.4
  2.7 2.5 %collective-permute-start.1 = (bf16[16,8192]{1,0:T(8,128)(2,1)}, bf16[16,8192]{1,0:T(8,128)(2,1)}, u32[]{:S(2)}, u32[]{:S(2)}) collective-permute-start(bf16[16,8192]{1,0:T(8,128)(2,1)} %get-tuple-element.14), channel_id=1, source_target_pairs={{0,4},{2,6},{4,0},{6,2},{1,5},{3,7},{5,1},{7,3},{8,12},{10,14},{12... | collective-permute-start | bytes 786440 | tf_op jit(solution)/shard_map/ppermute | solution.py:35
  5.3 6.3 %constant_dynamic-slice_fusion.3 = (bf16[128,8192]{1,0:T(8,128)(2,1)S(1)}, bf16[128,8192]{1,0:T(8,128)(2,1)}, bf16[128,8192]{1,0:T(8,128)(2,1)}, bf16[128,8192]{1,0:T(8,128)(2,1)}) fusion(bf16[128,32768]{1,0:T(8,128)(2,1)} %param.6, s32[]{:T(128)S(6)} %select_n.76, s32[]{:T(128)S(6)} %select_n.78, s32[]{:T(128)S(6)} %select_n.82, s32[]{:T(128)S(6)} %select_n.80), kind=kLoop, calls=%fused_computation.137 | loop fusion | bytes 16777232 | tf_op jit(solution)/shard_map/dynamic_slice | solution.py:47
  11.7 1.9 collective-permute-start.11
  13.6 1.0 constant_dynamic-update-slice_fusion.8
  14.6 1.0 constant_dynamic-update-slice_fusion.7
  15.6 2.2 %collective-permute-done.2 = bf16[16,8192]{1,0:T(8,128)(2,1)S(1)} collective-permute-done((bf16[16,8192]{1,0:T(8,128)(2,1)}, bf16[16,8192]{1,0:T(8,128)(2,1)S(1)}, u32[]{:S(2)}, u32[]{:S(2)}) %collective-permute-start.2) | collective-permute-done | bytes 262176 | tf_op jit(solution)/shard_map/ppermute | solution.py:35
  17.8 1.1 fusion.82
  18.9 3.6 %collective-permute-start.6 = (bf16[64,4096]{1,0:T(8,128)(2,1)}, bf16[64,4096]{1,0:T(8,128)(2,1)S(1)}, u32[]{:S(2)}, u32[]{:S(2)}) collective-permute-start(bf16[64,4096]{1,0:T(8,128)(2,1)} %get-tuple-element.10), channel_id=1, source_target_pairs={{0,24},{8,0},{16,8},{24,16},{1,25},{9,1},{17,9},{25,17},{2,26},{10... | collective-permute-start | bytes 1572872 | tf_op jit(solution)/shard_map/ppermute | solution.py:38
  22.9 1.3 dynamic_update_slice.92
  24.4 10.8 %collective-permute-done.6 = bf16[64,4096]{1,0:T(8,128)(2,1)S(1)} collective-permute-done((bf16[64,4096]{1,0:T(8,128)(2,1)}, bf16[64,4096]{1,0:T(8,128)(2,1)S(1)}, u32[]{:S(2)}, u32[]{:S(2)}) %collective-permute-start.6) | collective-permute-done | bytes 524320 | tf_op jit(solution)/shard_map/ppermute | solution.py:38
  35.2 4.2 %collective-permute-start.7 = (bf16[64,4096]{1,0:T(8,128)(2,1)S(1)}, bf16[64,4096]{1,0:T(8,128)(2,1)S(1)}, u32[]{:S(2)}, u32[]{:S(2)}) collective-permute-start(bf16[64,4096]{1,0:T(8,128)(2,1)S(1)} %collective-permute-done.6), channel_id=1, source_target_pairs={{0,24},{8,0},{16,8},{24,16},{1,25},{9,1},{17,9},{25,17},{2,26},{10... | collective-permute-start | bytes 1572872 | tf_op jit(solution)/shard_map/ppermute | solution.py:38
  39.4 7.8 %collective-permute-done.3 = bf16[64,4096]{1,0:T(8,128)(2,1)S(1)} collective-permute-done((bf16[64,4096]{1,0:T(8,128)(2,1)}, bf16[64,4096]{1,0:T(8,128)(2,1)S(1)}, u32[]{:S(2)}, u32[]{:S(2)}) %collective-permute-start.3) | collective-permute-done | bytes 524320 | tf_op jit(solution)/shard_map/ppermute | solution.py:38
  47.2 1.6 collective-permute-start.4
  48.8 9.6 %collective-permute-done.7 = bf16[64,4096]{1,0:T(8,128)(2,1)S(1)} collective-permute-done((bf16[64,4096]{1,0:T(8,128)(2,1)S(1)}, bf16[64,4096]{1,0:T(8,128)(2,1)S(1)}, u32[]{:S(2)}, u32[]{:S(2)}) %collective-permute-start.7) | collective-permute-done | bytes 524320 | tf_op jit(solution)/shard_map/ppermute | solution.py:38
  58.4 3.5 %collective-permute-start.8 = (bf16[64,4096]{1,0:T(8,128)(2,1)S(1)}, bf16[64,4096]{1,0:T(8,128)(2,1)S(1)}, u32[]{:S(2)}, u32[]{:S(2)}) collective-permute-start(bf16[64,4096]{1,0:T(8,128)(2,1)S(1)} %collective-permute-done.7), channel_id=1, source_target_pairs={{0,24},{8,0},{16,8},{24,16},{1,25},{9,1},{17,9},{25,17},{2,26},{10... | collective-permute-start | bytes 1572872 | tf_op jit(solution)/shard_map/ppermute | solution.py:38
  61.9 7.8 %collective-permute-done.4 = bf16[64,4096]{1,0:T(8,128)(2,1)S(1)} collective-permute-done((bf16[64,4096]{1,0:T(8,128)(2,1)S(1)}, bf16[64,4096]{1,0:T(8,128)(2,1)S(1)}, u32[]{:S(2)}, u32[]{:S(2)}) %collective-permute-start.4) | collective-permute-done | bytes 524320 | tf_op jit(solution)/shard_map/ppermute | solution.py:38
  69.7 1.6 collective-permute-start.5
  71.3 9.5 %collective-permute-done.8 = bf16[64,4096]{1,0:T(8,128)(2,1)S(1)} collective-permute-done((bf16[64,4096]{1,0:T(8,128)(2,1)S(1)}, bf16[64,4096]{1,0:T(8,128)(2,1)S(1)}, u32[]{:S(2)}, u32[]{:S(2)}) %collective-permute-start.8) | collective-permute-done | bytes 524320 | tf_op jit(solution)/shard_map/ppermute | solution.py:38
  80.9 11.0 %collective-permute-done.5 = bf16[64,4096]{1,0:T(8,128)(2,1)S(1)} collective-permute-done((bf16[64,4096]{1,0:T(8,128)(2,1)S(1)}, bf16[64,4096]{1,0:T(8,128)(2,1)S(1)}, u32[]{:S(2)}, u32[]{:S(2)}) %collective-permute-start.5) | collective-permute-done | bytes 524320 | tf_op jit(solution)/shard_map/ppermute | solution.py:38
  92.0 1.9 fusion.37
  93.9 2.0 convolution_add_fusion.14
  95.9 1.9 fusion.34
  97.9 2.0 convolution_add_fusion.13
  99.8 1.6 collective-permute-start.12
  101.4 6.4 %collective-permute-done.13 = bf16[128,8192]{1,0:T(8,128)(2,1)} collective-permute-done((bf16[128,8192]{1,0:T(8,128)(2,1)}, bf16[128,8192]{1,0:T(8,128)(2,1)}, u32[]{:S(2)}, u32[]{:S(2)}) %collective-permute-start.13) | collective-permute-done | bytes 2097184 | tf_op jit(solution)/shard_map/ppermute | solution.py:35
  107.8 1.9 fusion.31
  109.7 2.0 convolution_add_fusion.12
  111.7 1.9 collective-permute-start.14
  113.6 1.9 fusion.40
  115.5 1.8 collective-permute-done.14
  117.3 2.0 fusion.46
  119.3 1.1 collective-permute-start.15
  121.1 3.8 %collective-permute-done.15 = f32[256,128]{1,0:T(8,128)S(1)} collective-permute-done((f32[256,128]{1,0:T(8,128)S(1)}, f32[256,128]{1,0:T(8,128)S(1)}, u32[]{:S(2)}, u32[]{:S(2)}) %collective-permute-start.15) | collective-permute-done | bytes 131104 | tf_op jit(solution)/shard_map/ppermute | solution.py:35
  125.3 1.5 collective-permute-start.17
  127.1 3.8 %pad_maximum_fusion = bf16[512,8192]{1,0:T(8,128)(2,1)S(1)} fusion(bf16[128,8192]{1,0:T(8,128)(2,1)} %collective-permute-done.13, bf16[128,8192]{1,0:T(8,128)(2,1)} %collective-permute-done.11, bf16[128,8192]{1,0:T(8,128)(2,1)} %collective-permute-done.9, bf16[128,8192]{1,0:T(8,128)(2,1)S(1)} %get-tuple-element.5), kind=kLoop, calls=%fused_computation | loop fusion | flops 33554432 | bytes 16777216 | tf_op jit(solution)/shard_map/concatenate | solution.py:61
  132.8 3.7 %collective-permute-start.31 = (bf16[64,2048]{1,0:T(8,128)(2,1)S(1)}, bf16[64,2048]{1,0:T(8,128)(2,1)S(1)}, u32[]{:S(2)}, u32[]{:S(2)}) collective-permute-start(bf16[64,2048]{1,0:T(8,128)(2,1)S(1)} %convolution_convert_fusion), channel_id=1, source_target_pairs={{0,24},{8,0},{16,8},{24,16},{1,25},{9,1},{17,9},{25,17},{2,26},{10... | collective-permute-start | bytes 786440 | tf_op jit(solution)/shard_map/ppermute | solution.py:38
  136.4 3.8 %collective-permute-start.22 = (bf16[64,2048]{1,0:T(8,128)(2,1)S(1)}, bf16[64,2048]{1,0:T(8,128)(2,1)S(1)}, u32[]{:S(2)}, u32[]{:S(2)}) collective-permute-start(bf16[64,2048]{1,0:T(8,128)(2,1)S(1)} %convolution_convert_fusion.2), channel_id=1, source_target_pairs={{0,24},{8,0},{16,8},{24,16},{1,25},{9,1},{17,9},{25,17},{2,26},{10... | collective-permute-start | bytes 786440 | tf_op jit(solution)/shard_map/ppermute | solution.py:38
  140.9 2.3 %collective-permute-done.31 = bf16[64,2048]{1,0:T(8,128)(2,1)S(1)} collective-permute-done((bf16[64,2048]{1,0:T(8,128)(2,1)S(1)}, bf16[64,2048]{1,0:T(8,128)(2,1)S(1)}, u32[]{:S(2)}, u32[]{:S(2)}) %collective-permute-start.31) | collective-permute-done | bytes 262176 | tf_op jit(solution)/shard_map/ppermute | solution.py:38
  143.7 4.5 %collective-permute-start.32 = (bf16[64,2048]{1,0:T(8,128)(2,1)S(1)}, bf16[64,2048]{1,0:T(8,128)(2,1)S(1)}, u32[]{:S(2)}, u32[]{:S(2)}) collective-permute-start(bf16[64,2048]{1,0:T(8,128)(2,1)S(1)} %fusion.11), channel_id=1, source_target_pairs={{0,24},{8,0},{16,8},{24,16},{1,25},{9,1},{17,9},{25,17},{2,26},{10... | collective-permute-start | bytes 786440 | tf_op jit(solution)/shard_map/ppermute | solution.py:38
  148.2 1.5 collective-permute-done.28
  150.2 1.6 collective-permute-start.29
  151.8 2.6 %collective-permute-done.22 = bf16[64,2048]{1,0:T(8,128)(2,1)S(1)} collective-permute-done((bf16[64,2048]{1,0:T(8,128)(2,1)S(1)}, bf16[64,2048]{1,0:T(8,128)(2,1)S(1)}, u32[]{:S(2)}, u32[]{:S(2)}) %collective-permute-start.22) | collective-permute-done | bytes 262176 | tf_op jit(solution)/shard_map/ppermute | solution.py:38
  154.9 4.3 %collective-permute-start.23 = (bf16[64,2048]{1,0:T(8,128)(2,1)S(1)}, bf16[64,2048]{1,0:T(8,128)(2,1)S(1)}, u32[]{:S(2)}, u32[]{:S(2)}) collective-permute-start(bf16[64,2048]{1,0:T(8,128)(2,1)S(1)} %fusion.5), channel_id=1, source_target_pairs={{0,24},{8,0},{16,8},{24,16},{1,25},{9,1},{17,9},{25,17},{2,26},{10... | collective-permute-start | bytes 786440 | tf_op jit(solution)/shard_map/ppermute | solution.py:38
  159.3 1.7 collective-permute-done.19
  161.5 1.6 collective-permute-start.20
  163.1 2.6 %collective-permute-done.32 = bf16[64,2048]{1,0:T(8,128)(2,1)S(1)} collective-permute-done((bf16[64,2048]{1,0:T(8,128)(2,1)S(1)}, bf16[64,2048]{1,0:T(8,128)(2,1)S(1)}, u32[]{:S(2)}, u32[]{:S(2)}) %collective-permute-start.32) | collective-permute-done | bytes 262176 | tf_op jit(solution)/shard_map/ppermute | solution.py:38
  166.3 4.3 %collective-permute-start.33 = (bf16[64,2048]{1,0:T(8,128)(2,1)S(1)}, bf16[64,2048]{1,0:T(8,128)(2,1)S(1)}, u32[]{:S(2)}, u32[]{:S(2)}) collective-permute-start(bf16[64,2048]{1,0:T(8,128)(2,1)S(1)} %fusion.10), channel_id=1, source_target_pairs={{0,24},{8,0},{16,8},{24,16},{1,25},{9,1},{17,9},{25,17},{2,26},{10... | collective-permute-start | bytes 786440 | tf_op jit(solution)/shard_map/ppermute | solution.py:38
  170.6 1.6 collective-permute-done.29
  172.8 1.6 collective-permute-start.30
  174.5 2.5 %collective-permute-done.23 = bf16[64,2048]{1,0:T(8,128)(2,1)S(1)} collective-permute-done((bf16[64,2048]{1,0:T(8,128)(2,1)S(1)}, bf16[64,2048]{1,0:T(8,128)(2,1)S(1)}, u32[]{:S(2)}, u32[]{:S(2)}) %collective-permute-start.23) | collective-permute-done | bytes 262176 | tf_op jit(solution)/shard_map/ppermute | solution.py:38
  177.6 4.3 %collective-permute-start.24 = (bf16[64,2048]{1,0:T(8,128)(2,1)S(1)}, bf16[64,2048]{1,0:T(8,128)(2,1)S(1)}, u32[]{:S(2)}, u32[]{:S(2)}) collective-permute-start(bf16[64,2048]{1,0:T(8,128)(2,1)S(1)} %fusion.4), channel_id=1, source_target_pairs={{0,24},{8,0},{16,8},{24,16},{1,25},{9,1},{17,9},{25,17},{2,26},{10... | collective-permute-start | bytes 786440 | tf_op jit(solution)/shard_map/ppermute | solution.py:38
  181.9 1.6 collective-permute-done.20
  184.1 1.6 collective-permute-start.21
  185.7 13.8 %collective-permute-done.24 = bf16[64,2048]{1,0:T(8,128)(2,1)S(1)} collective-permute-done((bf16[64,2048]{1,0:T(8,128)(2,1)S(1)}, bf16[64,2048]{1,0:T(8,128)(2,1)S(1)}, u32[]{:S(2)}, u32[]{:S(2)}) %collective-permute-start.24) | collective-permute-done | bytes 262176 | tf_op jit(solution)/shard_map/ppermute | solution.py:38
  200.1 5.4 %collective-permute-done.21 = bf16[64,2048]{1,0:T(8,128)(2,1)S(1)} collective-permute-done((bf16[64,2048]{1,0:T(8,128)(2,1)S(1)}, bf16[64,2048]{1,0:T(8,128)(2,1)S(1)}, u32[]{:S(2)}, u32[]{:S(2)}) %collective-permute-start.21) | collective-permute-done | bytes 262176 | tf_op jit(solution)/shard_map/ppermute | solution.py:38
  206.1 1.5 collective-permute-start.26
  209.4 1.4 collective-permute-start.35
  211.2 1.3 collective-permute-done.26
  212.5 1.7 collective-permute-done.27
  214.4 3.8 %collective-permute-done.35 = bf16[16,4096]{1,0:T(8,128)(2,1)S(1)} collective-permute-done((bf16[16,4096]{1,0:T(8,128)(2,1)S(1)}, bf16[16,4096]{1,0:T(8,128)(2,1)S(1)}, u32[]{:S(2)}, u32[]{:S(2)}) %collective-permute-start.35) | collective-permute-done | bytes 131104 | tf_op jit(solution)/shard_map/ppermute | solution.py:35
  218.2 1.7 collective-permute-done.36
  219.9 1.0 copy-done.2
  220.8 0.6 slice_dynamic-update-slice_fusion
  (87 shorter events, 13.3 us)
Async XLA Ops:
  0.0 22.5 %copy-start = (f32[16,8,8]{0,2,1:T(8,128)S(1)}, f32[16,8,8]{0,2,1:T(8,128)}, u32[]{:S(2)}) copy-start(f32[16,8,8]{0,2,1:T(8,128)} %param.7) | copy-start | bytes 12292
  2.2 11.4 %collective-permute-start = (bf16[16,8192]{1,0:T(8,128)(2,1)}, bf16[16,8192]{1,0:T(8,128)(2,1)}, u32[]{:S(2)}, u32[]{:S(2)}) collective-permute-start(bf16[16,8192]{1,0:T(8,128)(2,1)} %get-tuple-element.12), channel_id=1, source_target_pairs={{0,2},{2,0},{4,6},{6,4},{1,3},{3,1},{5,7},{7,5},{8,10},{10,8},{12,... | collective-permute-start | bytes 786440 | tf_op jit(solution)/shard_map/ppermute | solution.py:35
  2.7 11.9 %collective-permute-start.1 = (bf16[16,8192]{1,0:T(8,128)(2,1)}, bf16[16,8192]{1,0:T(8,128)(2,1)}, u32[]{:S(2)}, u32[]{:S(2)}) collective-permute-start(bf16[16,8192]{1,0:T(8,128)(2,1)} %get-tuple-element.14), channel_id=1, source_target_pairs={{0,4},{2,6},{4,0},{6,2},{1,5},{3,7},{5,1},{7,3},{8,12},{10,14},{12... | collective-permute-start | bytes 786440 | tf_op jit(solution)/shard_map/ppermute | solution.py:35
  5.2 12.6 %collective-permute-start.2 = (bf16[16,8192]{1,0:T(8,128)(2,1)}, bf16[16,8192]{1,0:T(8,128)(2,1)S(1)}, u32[]{:S(2)}, u32[]{:S(2)}) collective-permute-start(bf16[16,8192]{1,0:T(8,128)(2,1)} %get-tuple-element.11), channel_id=1, source_target_pairs={{0,6},{2,4},{4,2},{6,0},{1,7},{3,5},{5,3},{7,1},{8,14},{10,12},{12... | collective-permute-start | bytes 786440 | tf_op jit(solution)/shard_map/ppermute | solution.py:35
  11.6 10.9 %copy-start.4 = (s32[16]{0:T(128)S(1)}, s32[16]{0:T(128)}, u32[]{:S(2)}) copy-start(s32[16]{0:T(128)} %param.9) | copy-start | bytes 196
  11.6 10.9 %copy-start.3 = (s32[16]{0:T(128)S(1)}, s32[16]{0:T(128)}, u32[]{:S(2)}) copy-start(s32[16]{0:T(128)} %param.8) | copy-start | bytes 196
  11.6 80.4 %collective-permute-start.9 = (bf16[128,8192]{1,0:T(8,128)(2,1)}, bf16[128,8192]{1,0:T(8,128)(2,1)}, u32[]{:S(2)}, u32[]{:S(2)}) collective-permute-start(bf16[128,8192]{1,0:T(8,128)(2,1)} %get-tuple-element.6), channel_id=1, source_target_pairs={{0,2},{2,0},{4,6},{6,4},{1,3},{3,1},{5,7},{7,5},{8,10},{10,8},{12,... | collective-permute-start | bytes 6291464 | tf_op jit(solution)/shard_map/ppermute | solution.py:35
  11.7 84.2 %collective-permute-start.11 = (bf16[128,8192]{1,0:T(8,128)(2,1)}, bf16[128,8192]{1,0:T(8,128)(2,1)}, u32[]{:S(2)}, u32[]{:S(2)}) collective-permute-start(bf16[128,8192]{1,0:T(8,128)(2,1)} %get-tuple-element.8), channel_id=1, source_target_pairs={{0,4},{2,6},{4,0},{6,2},{1,5},{3,7},{5,1},{7,3},{8,12},{10,14},{12... | collective-permute-start | bytes 6291464 | tf_op jit(solution)/shard_map/ppermute | solution.py:35
  13.6 94.2 %collective-permute-start.13 = (bf16[128,8192]{1,0:T(8,128)(2,1)}, bf16[128,8192]{1,0:T(8,128)(2,1)}, u32[]{:S(2)}, u32[]{:S(2)}) collective-permute-start(bf16[128,8192]{1,0:T(8,128)(2,1)} %get-tuple-element.7), channel_id=1, source_target_pairs={{0,6},{2,4},{4,2},{6,0},{1,7},{3,5},{5,3},{7,1},{8,14},{10,12},{12... | collective-permute-start | bytes 6291464 | tf_op jit(solution)/shard_map/ppermute | solution.py:35
  18.9 5.3 %copy-start.1 = (bf16[64,4096]{1,0:T(8,128)(2,1)S(1)}, bf16[64,4096]{1,0:T(8,128)(2,1)}, u32[]{:S(2)}) copy-start(bf16[64,4096]{1,0:T(8,128)(2,1)} %get-tuple-element.9) | copy-start | bytes 1572868
  18.9 16.3 %collective-permute-start.6 = (bf16[64,4096]{1,0:T(8,128)(2,1)}, bf16[64,4096]{1,0:T(8,128)(2,1)S(1)}, u32[]{:S(2)}, u32[]{:S(2)}) collective-permute-start(bf16[64,4096]{1,0:T(8,128)(2,1)} %get-tuple-element.10), channel_id=1, source_target_pairs={{0,24},{8,0},{16,8},{24,16},{1,25},{9,1},{17,9},{25,17},{2,26},{10... | collective-permute-start | bytes 1572872 | tf_op jit(solution)/shard_map/ppermute | solution.py:38
  22.8 24.4 %collective-permute-start.3 = (bf16[64,4096]{1,0:T(8,128)(2,1)}, bf16[64,4096]{1,0:T(8,128)(2,1)S(1)}, u32[]{:S(2)}, u32[]{:S(2)}) collective-permute-start(bf16[64,4096]{1,0:T(8,128)(2,1)} %get-tuple-element.9), channel_id=1, source_target_pairs={{0,8},{8,16},{16,24},{24,0},{1,9},{9,17},{17,25},{25,1},{2,10},{10... | collective-permute-start | bytes 1572872 | tf_op jit(solution)/shard_map/ppermute | solution.py:38
  35.2 23.2 %collective-permute-start.7 = (bf16[64,4096]{1,0:T(8,128)(2,1)S(1)}, bf16[64,4096]{1,0:T(8,128)(2,1)S(1)}, u32[]{:S(2)}, u32[]{:S(2)}) collective-permute-start(bf16[64,4096]{1,0:T(8,128)(2,1)S(1)} %collective-permute-done.6), channel_id=1, source_target_pairs={{0,24},{8,0},{16,8},{24,16},{1,25},{9,1},{17,9},{25,17},{2,26},{10... | collective-permute-start | bytes 1572872 | tf_op jit(solution)/shard_map/ppermute | solution.py:38
  47.2 22.5 %collective-permute-start.4 = (bf16[64,4096]{1,0:T(8,128)(2,1)S(1)}, bf16[64,4096]{1,0:T(8,128)(2,1)S(1)}, u32[]{:S(2)}, u32[]{:S(2)}) collective-permute-start(bf16[64,4096]{1,0:T(8,128)(2,1)S(1)} %collective-permute-done.3), channel_id=1, source_target_pairs={{0,8},{8,16},{16,24},{24,0},{1,9},{9,17},{17,25},{25,1},{2,10},{10... | collective-permute-start | bytes 1572872 | tf_op jit(solution)/shard_map/ppermute | solution.py:38
  58.4 22.5 %collective-permute-start.8 = (bf16[64,4096]{1,0:T(8,128)(2,1)S(1)}, bf16[64,4096]{1,0:T(8,128)(2,1)S(1)}, u32[]{:S(2)}, u32[]{:S(2)}) collective-permute-start(bf16[64,4096]{1,0:T(8,128)(2,1)S(1)} %collective-permute-done.7), channel_id=1, source_target_pairs={{0,24},{8,0},{16,8},{24,16},{1,25},{9,1},{17,9},{25,17},{2,26},{10... | collective-permute-start | bytes 1572872 | tf_op jit(solution)/shard_map/ppermute | solution.py:38
  69.7 22.2 %collective-permute-start.5 = (bf16[64,4096]{1,0:T(8,128)(2,1)S(1)}, bf16[64,4096]{1,0:T(8,128)(2,1)S(1)}, u32[]{:S(2)}, u32[]{:S(2)}) collective-permute-start(bf16[64,4096]{1,0:T(8,128)(2,1)S(1)} %collective-permute-done.4), channel_id=1, source_target_pairs={{0,8},{8,16},{16,24},{24,0},{1,9},{9,17},{17,25},{25,1},{2,10},{10... | collective-permute-start | bytes 1572872 | tf_op jit(solution)/shard_map/ppermute | solution.py:38
  95.9 19.7 %collective-permute-start.10 = (f32[256,128]{1,0:T(8,128)S(1)}, f32[256,128]{1,0:T(8,128)S(1)}, u32[]{:S(2)}, u32[]{:S(2)}) collective-permute-start(f32[256,128]{1,0:T(8,128)S(1)} %convolution_add_fusion.14), channel_id=1, source_target_pairs={{0,2},{2,0},{4,6},{6,4},{1,3},{3,1},{5,7},{7,5},{8,10},{10,8},{12,... | collective-permute-start | bytes 393224 | tf_op jit(solution)/shard_map/ppermute | solution.py:35
  99.8 15.7 %collective-permute-start.12 = (f32[256,128]{1,0:T(8,128)S(1)}, f32[256,128]{1,0:T(8,128)S(1)}, u32[]{:S(2)}, u32[]{:S(2)}) collective-permute-start(f32[256,128]{1,0:T(8,128)S(1)} %convolution_add_fusion.13), channel_id=1, source_target_pairs={{0,4},{2,6},{4,0},{6,2},{1,5},{3,7},{5,1},{7,3},{8,12},{10,14},{12... | collective-permute-start | bytes 393224 | tf_op jit(solution)/shard_map/ppermute | solution.py:35
  111.7 5.6 %collective-permute-start.14 = (f32[256,128]{1,0:T(8,128)S(1)}, f32[256,128]{1,0:T(8,128)S(1)}, u32[]{:S(2)}, u32[]{:S(2)}) collective-permute-start(f32[256,128]{1,0:T(8,128)S(1)} %convolution_add_fusion.12), channel_id=1, source_target_pairs={{0,6},{2,4},{4,2},{6,0},{1,7},{3,5},{5,3},{7,1},{8,14},{10,12},{12... | collective-permute-start | bytes 393224 | tf_op jit(solution)/shard_map/ppermute | solution.py:35
  119.3 5.6 %collective-permute-start.15 = (f32[256,128]{1,0:T(8,128)S(1)}, f32[256,128]{1,0:T(8,128)S(1)}, u32[]{:S(2)}, u32[]{:S(2)}) collective-permute-start(f32[256,128]{1,0:T(8,128)S(1)} %fusion.46), channel_id=1, source_target_pairs={{0,1},{1,0},{2,3},{3,2},{4,5},{5,4},{6,7},{7,6},{8,9},{9,8},{10,11... | collective-permute-start | bytes 393224 | tf_op jit(solution)/shard_map/ppermute | solution.py:35
  125.2 5.7 %collective-permute-start.16 = (bf16[256,128]{0,1:T(8,128)(2,1)S(1)}, bf16[256,128]{0,1:T(8,128)(2,1)S(1)}, u32[]{:S(2)}, u32[]{:S(2)}) collective-permute-start(bf16[256,128]{0,1:T(8,128)(2,1)S(1)} %convolution_convert_fusion.4), channel_id=1, source_target_pairs={{0,2},{2,0},{4,6},{6,4},{1,3},{3,1},{5,7},{7,5},{8,10},{10,8},{12,... | collective-permute-start | bytes 196616 | tf_op jit(solution)/shard_map/ppermute | solution.py:35
  125.3 5.7 %collective-permute-start.17 = (bf16[256,128]{0,1:T(8,128)(2,1)S(1)}, bf16[256,128]{0,1:T(8,128)(2,1)S(1)}, u32[]{:S(2)}, u32[]{:S(2)}) collective-permute-start(bf16[256,128]{0,1:T(8,128)(2,1)S(1)} %convolution_convert_fusion.4), channel_id=1, source_target_pairs={{0,4},{2,6},{4,0},{6,2},{1,5},{3,7},{5,1},{7,3},{8,12},{10,14},{12... | collective-permute-start | bytes 196616 | tf_op jit(solution)/shard_map/ppermute | solution.py:35
  126.7 4.2 %collective-permute-start.18 = (bf16[256,128]{0,1:T(8,128)(2,1)S(1)}, bf16[256,128]{0,1:T(8,128)(2,1)S(1)}, u32[]{:S(2)}, u32[]{:S(2)}) collective-permute-start(bf16[256,128]{0,1:T(8,128)(2,1)S(1)} %convolution_convert_fusion.4), channel_id=1, source_target_pairs={{0,6},{2,4},{4,2},{6,0},{1,7},{3,5},{5,3},{7,1},{8,14},{10,12},{12... | collective-permute-start | bytes 196616 | tf_op jit(solution)/shard_map/ppermute | solution.py:35
  132.8 10.4 %collective-permute-start.31 = (bf16[64,2048]{1,0:T(8,128)(2,1)S(1)}, bf16[64,2048]{1,0:T(8,128)(2,1)S(1)}, u32[]{:S(2)}, u32[]{:S(2)}) collective-permute-start(bf16[64,2048]{1,0:T(8,128)(2,1)S(1)} %convolution_convert_fusion), channel_id=1, source_target_pairs={{0,24},{8,0},{16,8},{24,16},{1,25},{9,1},{17,9},{25,17},{2,26},{10... | collective-permute-start | bytes 786440 | tf_op jit(solution)/shard_map/ppermute | solution.py:38
  136.4 13.3 %collective-permute-start.28 = (bf16[64,2048]{1,0:T(8,128)(2,1)S(1)}, bf16[64,2048]{1,0:T(8,128)(2,1)S(1)}, u32[]{:S(2)}, u32[]{:S(2)}) collective-permute-start(bf16[64,2048]{1,0:T(8,128)(2,1)S(1)} %convolution_convert_fusion.1), channel_id=1, source_target_pairs={{0,8},{8,16},{16,24},{24,0},{1,9},{9,17},{17,25},{25,1},{2,10},{10... | collective-permute-start | bytes 786440 | tf_op jit(solution)/shard_map/ppermute | solution.py:38
  136.4 18.0 %collective-permute-start.22 = (bf16[64,2048]{1,0:T(8,128)(2,1)S(1)}, bf16[64,2048]{1,0:T(8,128)(2,1)S(1)}, u32[]{:S(2)}, u32[]{:S(2)}) collective-permute-start(bf16[64,2048]{1,0:T(8,128)(2,1)S(1)} %convolution_convert_fusion.2), channel_id=1, source_target_pairs={{0,24},{8,0},{16,8},{24,16},{1,25},{9,1},{17,9},{25,17},{2,26},{10... | collective-permute-start | bytes 786440 | tf_op jit(solution)/shard_map/ppermute | solution.py:38
  140.8 20.1 %collective-permute-start.19 = (bf16[64,2048]{1,0:T(8,128)(2,1)S(1)}, bf16[64,2048]{1,0:T(8,128)(2,1)S(1)}, u32[]{:S(2)}, u32[]{:S(2)}) collective-permute-start(bf16[64,2048]{1,0:T(8,128)(2,1)S(1)} %convolution_convert_fusion.3), channel_id=1, source_target_pairs={{0,8},{8,16},{16,24},{24,0},{1,9},{9,17},{17,25},{25,1},{2,10},{10... | collective-permute-start | bytes 786440 | tf_op jit(solution)/shard_map/ppermute | solution.py:38
  143.7 22.0 %collective-permute-start.32 = (bf16[64,2048]{1,0:T(8,128)(2,1)S(1)}, bf16[64,2048]{1,0:T(8,128)(2,1)S(1)}, u32[]{:S(2)}, u32[]{:S(2)}) collective-permute-start(bf16[64,2048]{1,0:T(8,128)(2,1)S(1)} %fusion.11), channel_id=1, source_target_pairs={{0,24},{8,0},{16,8},{24,16},{1,25},{9,1},{17,9},{25,17},{2,26},{10... | collective-permute-start | bytes 786440 | tf_op jit(solution)/shard_map/ppermute | solution.py:38
  150.2 22.0 %collective-permute-start.29 = (bf16[64,2048]{1,0:T(8,128)(2,1)S(1)}, bf16[64,2048]{1,0:T(8,128)(2,1)S(1)}, u32[]{:S(2)}, u32[]{:S(2)}) collective-permute-start(bf16[64,2048]{1,0:T(8,128)(2,1)S(1)} %fusion.8), channel_id=1, source_target_pairs={{0,8},{8,16},{16,24},{24,0},{1,9},{9,17},{17,25},{25,1},{2,10},{10... | collective-permute-start | bytes 786440 | tf_op jit(solution)/shard_map/ppermute | solution.py:38
  154.9 22.0 %collective-permute-start.23 = (bf16[64,2048]{1,0:T(8,128)(2,1)S(1)}, bf16[64,2048]{1,0:T(8,128)(2,1)S(1)}, u32[]{:S(2)}, u32[]{:S(2)}) collective-permute-start(bf16[64,2048]{1,0:T(8,128)(2,1)S(1)} %fusion.5), channel_id=1, source_target_pairs={{0,24},{8,0},{16,8},{24,16},{1,25},{9,1},{17,9},{25,17},{2,26},{10... | collective-permute-start | bytes 786440 | tf_op jit(solution)/shard_map/ppermute | solution.py:38
  161.5 22.0 %collective-permute-start.20 = (bf16[64,2048]{1,0:T(8,128)(2,1)S(1)}, bf16[64,2048]{1,0:T(8,128)(2,1)S(1)}, u32[]{:S(2)}, u32[]{:S(2)}) collective-permute-start(bf16[64,2048]{1,0:T(8,128)(2,1)S(1)} %fusion.2), channel_id=1, source_target_pairs={{0,8},{8,16},{16,24},{24,0},{1,9},{9,17},{17,25},{25,1},{2,10},{10... | collective-permute-start | bytes 786440 | tf_op jit(solution)/shard_map/ppermute | solution.py:38
  166.3 41.6 %collective-permute-start.33 = (bf16[64,2048]{1,0:T(8,128)(2,1)S(1)}, bf16[64,2048]{1,0:T(8,128)(2,1)S(1)}, u32[]{:S(2)}, u32[]{:S(2)}) collective-permute-start(bf16[64,2048]{1,0:T(8,128)(2,1)S(1)} %fusion.10), channel_id=1, source_target_pairs={{0,24},{8,0},{16,8},{24,16},{1,25},{9,1},{17,9},{25,17},{2,26},{10... | collective-permute-start | bytes 786440 | tf_op jit(solution)/shard_map/ppermute | solution.py:38
  172.8 35.6 %collective-permute-start.30 = (bf16[64,2048]{1,0:T(8,128)(2,1)S(1)}, bf16[64,2048]{1,0:T(8,128)(2,1)S(1)}, u32[]{:S(2)}, u32[]{:S(2)}) collective-permute-start(bf16[64,2048]{1,0:T(8,128)(2,1)S(1)} %fusion.7), channel_id=1, source_target_pairs={{0,8},{8,16},{16,24},{24,0},{1,9},{9,17},{17,25},{25,1},{2,10},{10... | collective-permute-start | bytes 786440 | tf_op jit(solution)/shard_map/ppermute | solution.py:38
  177.6 22.0 %collective-permute-start.24 = (bf16[64,2048]{1,0:T(8,128)(2,1)S(1)}, bf16[64,2048]{1,0:T(8,128)(2,1)S(1)}, u32[]{:S(2)}, u32[]{:S(2)}) collective-permute-start(bf16[64,2048]{1,0:T(8,128)(2,1)S(1)} %fusion.4), channel_id=1, source_target_pairs={{0,24},{8,0},{16,8},{24,16},{1,25},{9,1},{17,9},{25,17},{2,26},{10... | collective-permute-start | bytes 786440 | tf_op jit(solution)/shard_map/ppermute | solution.py:38
  184.1 21.3 %collective-permute-start.21 = (bf16[64,2048]{1,0:T(8,128)(2,1)S(1)}, bf16[64,2048]{1,0:T(8,128)(2,1)S(1)}, u32[]{:S(2)}, u32[]{:S(2)}) collective-permute-start(bf16[64,2048]{1,0:T(8,128)(2,1)S(1)} %fusion.1), channel_id=1, source_target_pairs={{0,8},{8,16},{16,24},{24,0},{1,9},{9,17},{17,25},{25,1},{2,10},{10... | collective-permute-start | bytes 786440 | tf_op jit(solution)/shard_map/ppermute | solution.py:38
  206.0 5.0 %collective-permute-start.25 = (bf16[16,4096]{1,0:T(8,128)(2,1)S(1)}, bf16[16,4096]{1,0:T(8,128)(2,1)S(1)}, u32[]{:S(2)}, u32[]{:S(2)}) collective-permute-start(bf16[16,4096]{1,0:T(8,128)(2,1)S(1)} %get-tuple-element.21), channel_id=1, source_target_pairs={{0,2},{2,0},{4,6},{6,4},{1,3},{3,1},{5,7},{7,5},{8,10},{10,8},{12,... | collective-permute-start | bytes 393224 | tf_op jit(solution)/shard_map/ppermute | solution.py:35
  206.1 6.4 %collective-permute-start.26 = (bf16[16,4096]{1,0:T(8,128)(2,1)S(1)}, bf16[16,4096]{1,0:T(8,128)(2,1)S(1)}, u32[]{:S(2)}, u32[]{:S(2)}) collective-permute-start(bf16[16,4096]{1,0:T(8,128)(2,1)S(1)} %get-tuple-element.22), channel_id=1, source_target_pairs={{0,4},{2,6},{4,0},{6,2},{1,5},{3,7},{5,1},{7,3},{8,12},{10,14},{12... | collective-permute-start | bytes 393224 | tf_op jit(solution)/shard_map/ppermute | solution.py:35
  207.5 6.7 %collective-permute-start.27 = (bf16[16,4096]{1,0:T(8,128)(2,1)S(1)}, bf16[16,4096]{1,0:T(8,128)(2,1)S(1)}, u32[]{:S(2)}, u32[]{:S(2)}) collective-permute-start(bf16[16,4096]{1,0:T(8,128)(2,1)S(1)} %get-tuple-element.19), channel_id=1, source_target_pairs={{0,6},{2,4},{4,2},{6,0},{1,7},{3,5},{5,3},{7,1},{8,14},{10,12},{12... | collective-permute-start | bytes 393224 | tf_op jit(solution)/shard_map/ppermute | solution.py:35
  209.0 5.3 %collective-permute-start.34 = (bf16[16,4096]{1,0:T(8,128)(2,1)S(1)}, bf16[16,4096]{1,0:T(8,128)(2,1)S(1)}, u32[]{:S(2)}, u32[]{:S(2)}) collective-permute-start(bf16[16,4096]{1,0:T(8,128)(2,1)S(1)} %get-tuple-element.17), channel_id=1, source_target_pairs={{0,2},{2,0},{4,6},{6,4},{1,3},{3,1},{5,7},{7,5},{8,10},{10,8},{12,... | collective-permute-start | bytes 393224 | tf_op jit(solution)/shard_map/ppermute | solution.py:35
  209.4 8.7 %collective-permute-start.35 = (bf16[16,4096]{1,0:T(8,128)(2,1)S(1)}, bf16[16,4096]{1,0:T(8,128)(2,1)S(1)}, u32[]{:S(2)}, u32[]{:S(2)}) collective-permute-start(bf16[16,4096]{1,0:T(8,128)(2,1)S(1)} %get-tuple-element.18), channel_id=1, source_target_pairs={{0,4},{2,6},{4,0},{6,2},{1,5},{3,7},{5,1},{7,3},{8,12},{10,14},{12... | collective-permute-start | bytes 393224 | tf_op jit(solution)/shard_map/ppermute | solution.py:35
  211.0 8.9 %collective-permute-start.36 = (bf16[16,4096]{1,0:T(8,128)(2,1)S(1)}, bf16[16,4096]{1,0:T(8,128)(2,1)S(1)}, u32[]{:S(2)}, u32[]{:S(2)}) collective-permute-start(bf16[16,4096]{1,0:T(8,128)(2,1)S(1)} %get-tuple-element.15), channel_id=1, source_target_pairs={{0,6},{2,4},{4,2},{6,0},{1,7},{3,5},{5,3},{7,1},{8,14},{10,12},{12... | collective-permute-start | bytes 393224 | tf_op jit(solution)/shard_map/ppermute | solution.py:35
  219.9 1.0 copy-start.2
